TPU v7x, 32 devices: a whole 2x2x4 slice. The times are simulated.
32 devices in a mesh: row: 4 (over y, x), col: 8 (over z, core).
Axes of the slice: x: 2, y: 2, z: 4, core: 2. Of those that a mesh axis runs over, the one named last changes fastest.
Arguments:
- tiles: bfloat16 [1024, 256, 256], P(('row', 'col')), as said below
- tile_row: int32 [1024], P(('row', 'col')), may hold values from 0 to 31, as said below
- tile_col: int32 [1024], P(('row', 'col')), may hold values from 0 to 31, as said below
- label_class: int32 [8192], P(('row', 'col')), may hold values from -1 to 127, as said below
Outputs:
- scores: float32 [8192, 128], P(('row', 'col'))
- residual: float32 [8192, 128], P(('row', 'col'))
Inputs may be any that keep to these rules, and one draw needn't show every extreme that they name: `tiles`: Nonnegative. The tile of blocks (j, i) is the transpose of the tile of blocks (i, j); a tile on the diagonal is symmetric. No pair of blocks appears twice; the pair (j, i) is stored whenever (i, j) is. The device with row index r and col index c holds 32 tiles, all with tile_row // 8 == r and tile_col % 8 == c. `tile_col`: see tile_row. `label_class`: exactly 1024 nodes are labeled, and every class labels at least one node.
All inputs are finite; a program needn't handle non-finite values.
Results may differ from a plain program's by a relative error of at most 0.00062.
Values may be sent and summed in bfloat16 or wider, within the bound.
A program may use at most 64 MiB of HBM per device.

v0:
```python
import functools

import jax
import jax.numpy as jnp
from jax import lax
from jax.experimental import pallas as pl
from jax.experimental.pallas import tpu as pltpu
from jax.sharding import PartitionSpec as P

CLASSES = 128
ITERS = 3
PAD = 16
DEG = 8
UNROLL = 32
PARTS = 4


def each(count, body, unroll):
    if unroll:
        for n in range(count):
            body(n)
    else:
        def step(n, carry):
            body(n)
            return carry
        lax.fori_loop(0, count, step, 0)


def flip(index, mask):
    bit = 1
    result = index
    while bit <= mask:
        if mask & bit:
            result = result + bit * (1 - 2 * lax.rem(lax.div(index, bit), 2))
        bit *= 2
    return result


def kernel(
    R, C, pos, label_ref, tiles_hbm, x_out, r_out,
    tiles, lab, ag0, ag, acc0a, acc0b, acc, rs0a, rs0b, rs, st_ag, st_row, st_rs,
    degree, direction, image, residual, answer,
    tile_sem, lab_send, lab_recv, ag_send, ag_recv, st_send, st_recv,
    str_send, str_recv, rs_send, rs_recv,
):
    T, B = tiles_hbm.shape[0], tiles_hbm.shape[1]
    Z = C // 2
    K, H = CLASSES, CLASSES // 2
    unroll = R * C <= UNROLL
    row, col = lax.axis_index("row"), lax.axis_index("col")
    core = lax.rem(col, 2)
    peer = col + 1 - 2 * core
    pow2_z = Z & (Z - 1) == 0
    pow2_r = R & (R - 1) == 0
    assert pow2_z and pow2_r

    def col_partner(m):
        return flip(col, m)

    def row_partner(m):
        return flip(row, m)

    step = -(-T // PARTS)
    tile_copies = []
    for p in range(PARTS):
        lo, hi = p * step, min(T, (p + 1) * step)
        if lo < hi:
            cp = pltpu.make_async_copy(
                tiles_hbm.at[pl.ds(lo, hi - lo)], tiles.at[pl.ds(lo, hi - lo)], tile_sem.at[p]
            )
            cp.start()
            tile_copies.append(cp)
    if tiles.shape[0] > T:
        tiles[T] = jnp.zeros((B, B), jnp.bfloat16)

    barrier = pltpu.get_barrier_semaphore()
    for m in range(1, C):
        pl.semaphore_signal(
            barrier, inc=1, device_id={"col": col_partner(m)}, device_id_type=pl.DeviceIdType.MESH
        )
    for m in range(1, R):
        pl.semaphore_signal(
            barrier, inc=1, device_id={"row": row_partner(m)}, device_id_type=pl.DeviceIdType.MESH
        )
    mine = label_ref[...]
    lab[col] = jnp.broadcast_to(mine, (8, B))
    pl.semaphore_wait(barrier, C - 1 + R - 1)

    sent = []

    def send(src, dst, send_sem, recv_sem, where):
        cp = pltpu.make_async_remote_copy(
            src_ref=src, dst_ref=dst, send_sem=send_sem, recv_sem=recv_sem,
            device_id=where, device_id_type=pl.DeviceIdType.MESH,
        )
        cp.start()
        sent.append(cp)

    def arrive(dst, recv_sem):
        pltpu.make_async_remote_copy(
            src_ref=dst, dst_ref=dst, send_sem=tile_sem.at[0], recv_sem=recv_sem,
            device_id={"col": peer}, device_id_type=pl.DeviceIdType.MESH,
        ).wait_recv()

    def tile_at(source, k):
        return tiles[pos[source * R + k]]

    def scatter_start(t, total, slots, k_body):
        for m in range(R - 1, 0, -1):
            k = row_partner(m)
            k_body(k)
            send(total.at[k], slots.at[m - 1], rs_send.at[t, m], rs_recv.at[t, m], {"row": k})
        k_body(row)

    def scatter_end(t, total, slots):
        result = total[row]
        for m in range(1, R):
            arrive(slots.at[m - 1], rs_recv.at[t, m])
            result = result + slots[m - 1]
        return result

    def inner(a, b):
        product = a * b
        folded = product[:, :K]
        for lane in range(K, B, K):
            folded = folded + product[:, lane : lane + K]
        padded = jnp.concatenate([folded, jnp.zeros((K - H, K), jnp.float32)], axis=0)
        return jnp.sum(padded.T, axis=0, keepdims=True)

    def spread(values):
        square = jnp.broadcast_to(values, (K, K)).T[:H]
        return jnp.concatenate([square] * (B // K), axis=1)

    def stats_start(t, rows):
        st_ag[t, col] = jnp.concatenate(rows + [jnp.zeros((8 - len(rows), K), jnp.float32)], axis=0)
        for m in range(1, C):
            send(st_ag.at[t, col], st_ag.at[t, col], st_send.at[t, m], st_recv.at[t, col],
                 {"col": col_partner(m)})

    def stats_middle(t):
        for m in range(1, C):
            c = col_partner(m)
            arrive(st_ag.at[t, c], st_recv.at[t, c])
        st_row[t] = jnp.sum(st_ag[t], axis=0)
        for m in range(1, R):
            send(st_row.at[t], st_rs.at[t, row], str_send.at[t, m], str_recv.at[t, row],
                 {"row": row_partner(m)})
        st_rs[t, row] = st_row[t]

    def stats_end(t):
        for m in range(1, R):
            k = row_partner(m)
            arrive(st_rs.at[t, k], str_recv.at[t, k])
        return jnp.sum(st_rs[t], axis=0)

    for m in range(1, C):
        send(lab.at[col], lab.at[col], lab_send.at[m], lab_recv.at[col], {"col": col_partner(m)})
    class_axis = lax.broadcasted_iota(jnp.int32, (K, B), 0)
    ones = jnp.ones((PAD, B), jnp.bfloat16)

    def encode(c):
        hot = jnp.where(lab[c][0:1] == class_axis, 1.0, 0.0).astype(jnp.bfloat16)
        ag0[c] = jnp.concatenate([hot[:H], ones, hot[H:]], axis=0)

    encode(col)
    for m in range(1, C):
        c = col_partner(m)
        arrive(lab.at[c], lab_recv.at[c])
        encode(c)
    for cp in tile_copies:
        cp.wait()
    free = jnp.broadcast_to(mine, (H, B)) < 0

    def chain(h):
        lo, rows_in = (0, H + PAD) if h == 0 else (H + PAD, H)
        total, slots = (acc0a, rs0a) if h == 0 else (acc0b, rs0b)
        keep = total.shape[1]

        def first_products(k):
            def one(c, value):
                return value + jnp.dot(
                    ag0[c, lo : lo + rows_in], tile_at(c, k), preferred_element_type=jnp.float32
                )
            value = jnp.zeros((rows_in, B), jnp.float32)
            if unroll:
                for c in range(C):
                    value = one(c, value)
            else:
                value = lax.fori_loop(0, C, one, value)
            total[k] = value[:keep]

        scatter_start(h, total, slots, first_products)
        yield
        value = scatter_end(h, total, slots)
        if h == 0:
            degree[...] = value[H : H + DEG]
        rhs = jnp.where(free, value[:H], 0.0)
        answer[h] = jnp.zeros((H, B), jnp.float32)
        residual[h] = rhs
        direction[h] = rhs
        start = 2 * ITERS + h
        for iteration in range(ITERS):
            s = 2 * iteration + h
            last = iteration + 1 == ITERS
            ag[s, col] = direction[h].astype(jnp.bfloat16)
            own = ag.at[s, col]
            for o in range(1, Z):
                send(own, own, ag_send.at[s, o], ag_recv.at[s, col], {"col": col_partner(2 * o)})
            send(own, own, ag_send.at[s, 0], ag_recv.at[s, col], {"col": peer})
            if iteration == 0:
                stats_start(start, [inner(rhs, rhs)])

            def add(c, first=False):
                panel = ag[s, c]

                def one(k):
                    part = jnp.dot(panel, tile_at(c, k), preferred_element_type=jnp.float32)
                    acc[s, k] = part if first else acc[s, k] + part
                each(R, one, unroll)

            add(col, first=True)
            yield
            arrive(ag.at[s, peer], ag_recv.at[s, peer])
            add(peer)
            for o in range(1, Z):
                c = col_partner(2 * o)
                block = ag.at[s, c]
                arrive(block, ag_recv.at[s, c])
                send(block, block, ag_send.at[s, Z + o], ag_recv.at[s, c], {"col": peer})
                add(c)
            if iteration == 0:
                stats_middle(start)
            yield
            for o in range(1, Z):
                c = col_partner(2 * o + 1)
                arrive(ag.at[s, c], ag_recv.at[s, c])

            def finish(k):
                part = acc[s, k]
                for o in range(1, Z):
                    c = col_partner(2 * o + 1)
                    part = part + jnp.dot(ag[s, c], tile_at(c, k), preferred_element_type=jnp.float32)
                acc[s, k] = part

            scatter_start(2 + s, acc.at[s], rs.at[s], finish)
            yield
            mixed = scatter_end(2 + s, acc.at[s], rs.at[s])
            d, r = direction[h], residual[h]
            i = jnp.where(free, degree[0:1] * d - mixed, d)
            image[h] = i
            stats_start(s, [inner(d, i)] + ([] if last else [inner(r, i), inner(i, i)]))
            yield
            stats_middle(s)
            yield
            if iteration == 0:
                norm = stats_end(start)[0:1]
            sums = stats_end(s)
            alpha = norm / sums[0:1]
            wide = spread(alpha)
            d = direction[h]
            r = residual[h] - wide * image[h]
            x = answer[h] + wide * d
            if last:
                x_out[:, h * H : (h + 1) * H] = ((8.0 * K) * x).T
                r_out[:, h * H : (h + 1) * H] = r.T
            else:
                norm_next = norm - 2.0 * alpha * sums[1:2] + alpha * alpha * sums[2:3]
                direction[h] = r + spread(norm_next / norm) * d
                residual[h] = r
                answer[h] = x
                norm = norm_next

    running = [chain(0), chain(1)]
    while running:
        for one in list(running):
            if next(one, running) is running:
                running.remove(one)
    for cp in sent:
        cp.wait_send()


def solution(mesh):
    R, C = mesh.shape["row"], mesh.shape["col"]

    def shards(tiles, tile_row, tile_col, label_class):
        T, B = tiles.shape[0], tiles.shape[1]
        K, H = CLASSES, CLASSES // 2
        place = (tile_row % C) * R + tile_col // C
        slot = jnp.arange(R * C, dtype=jnp.int32)
        index = jnp.arange(T, dtype=jnp.int32)
        held = T if T == R * C else T + 1
        pos = jnp.max(jnp.where(place[None, :] == slot[:, None], T - index[None, :], T + 1 - held), axis=1)
        pos = T - pos
        f32, bf16 = jnp.float32, jnp.bfloat16
        dma = pltpu.SemaphoreType.DMA
        vmem = pl.BlockSpec(memory_space=pltpu.VMEM)
        node = pltpu.VMEM((2, H, B), f32)
        return pl.pallas_call(
            functools.partial(kernel, R, C),
            out_shape=(jax.ShapeDtypeStruct((B, K), f32), jax.ShapeDtypeStruct((B, K), f32)),
            in_specs=[
                pl.BlockSpec(memory_space=pltpu.SMEM),
                vmem,
                pl.BlockSpec(memory_space=pl.ANY),
            ],
            out_specs=(vmem, vmem),
            scratch_shapes=[
                pltpu.VMEM((held, B, B), bf16),
                pltpu.VMEM((C, 8, B), jnp.int32),
                pltpu.VMEM((C, K + PAD, B), bf16),
                pltpu.VMEM((2 * ITERS, C, H, B), bf16),
                pltpu.VMEM((R, H + DEG, B), f32),
                pltpu.VMEM((R, H, B), f32),
                pltpu.VMEM((2 * ITERS, R, H, B), f32),
                pltpu.VMEM((R - 1, H + DEG, B), f32),
                pltpu.VMEM((R - 1, H, B), f32),
                pltpu.VMEM((2 * ITERS, R - 1, H, B), f32),
                pltpu.VMEM((2 * ITERS + 2, C, 8, K), f32),
                pltpu.VMEM((2 * ITERS + 2, 8, K), f32),
                pltpu.VMEM((2 * ITERS + 2, R, 8, K), f32),
                pltpu.VMEM((DEG, B), f32),
                node, node, node, node,
                dma((PARTS,)),
                dma((C,)), dma((C,)),
                dma((2 * ITERS, C)), dma((2 * ITERS, C)),
                dma((2 * ITERS + 2, C)), dma((2 * ITERS + 2, C)),
                dma((2 * ITERS + 2, R)), dma((2 * ITERS + 2, R)),
                dma((2 * ITERS + 2, R)), dma((2 * ITERS + 2, R)),
            ],
            compiler_params=pltpu.CompilerParams(
                collective_id=0, has_side_effects=True, vmem_limit_bytes=63 * 1024 * 1024
            ),
        )(pos.astype(jnp.int32), label_class.reshape(1, B), tiles)

    placed = (P(("row", "col"), None, None),) + (P(("row", "col")),) * 3
    return jax.shard_map(
        shards,
        mesh=mesh,
        in_specs=placed,
        out_specs=(P(("row", "col"), None), P(("row", "col"), None)),
        check_vma=False,
    )
```

profile of v0, /device:TPU:0, one launch (start us, length us, event | category | flops | bytes accessed | tf_op | source)
XLA Modules:
  0.0 90.0 jit_solution(2646302820275178186)
XLA Ops:
  0.6 0.7 fusion.1
  1.3 0.1 select_reduce_fusion
  1.4 0.5 broadcast_subtract_fusion.pos
  1.9 84.9 %shard_map.59 = (f32[256,128]{1,0:T(8,128)}, f32[256,128]{1,0:T(8,128)}) custom-call(s32[32]{0:T(128)} %broadcast_subtract_fusion.pos, s32[1,256]{1,0:T(1,128)} %bitcast.1, bf16[32,256,256]{2,1,0:T(8,128)(2,1)} %tiles_hbm.1), custom_call_target="tpu_custom_call" | custom-call | tf_op jit(solution)/shard_map/pallas_call | solution.py:298
  86.9 1.6 %copy.8 = f32[256,128]{1,0:T(8,128)} copy(f32[256,128]{1,0:T(8,128)} %get-tuple-element.6) | data formatting | bytes 262144
  88.4 1.6 %copy.9 = f32[256,128]{1,0:T(8,128)} copy(f32[256,128]{1,0:T(8,128)} %get-tuple-element.7) | data formatting | bytes 262144
where the time goes:
time: 90.2 us; the launch traced here: 90 us
  Pallas kernels  84.9 us (94%)
  local copies, waits for them, and re-layouts  3.14 us (3%)
  other arithmetic  1.32 us (1%)
    pallas_call x1, Pallas kernels, shards(): pl.pallas_call(functools.partial(kernel, R, C), out_shape=(jax.ShapeDtype...  84.9 us
    unnamed x2, local copies, waits for them, and re-layouts  3.14 us

commit v1 on v0

v1 whole, which is shorter than its diff:
```python
import functools

import jax
import jax.numpy as jnp
from jax import lax
from jax.experimental import pallas as pl
from jax.experimental.pallas import tpu as pltpu
from jax.sharding import PartitionSpec as P

CLASSES = 128
ITERS = 3
PAD = 16
DEG = 8
UNROLL = 32
PARTS = 4
CHAINS = 4
LIMIT = 32700.0
OFFSET = 1.4
NEAR, FAR, READY, PERIOD = 2.8, 5.0, 6.5, 10.2


def flip(index, mask):
    bit = 1
    result = index
    while bit <= mask:
        if mask & bit:
            result = result + bit * (1 - 2 * lax.rem(lax.div(index, bit), 2))
        bit *= 2
    return result


def kernel(
    R, C, pos, label_ref, tiles_hbm, x_out, r_out,
    tiles, lab, hot, acc0, rs0, code, unit, panel, rep_r, rep_p, acc, rs, st_a, st_c,
    degree, direction, image, residual, answer,
    tile_sem, lab_send, lab_recv, code_send, code_recv, unit_send, unit_recv, deg_send, rs0_send, rs0_recv, rs_send, rs_recv,
    sta_send, sta_recv, stc_send, stc_recv,
):
    T, B = tiles_hbm.shape[0], tiles_hbm.shape[1]
    Z = C // 2
    K, H = CLASSES, CLASSES // CHAINS
    Q = K // H
    G = H // 2
    f32, bf16, i32 = jnp.float32, jnp.bfloat16, jnp.int32
    unroll = R * C <= UNROLL
    row, col = lax.axis_index("row"), lax.axis_index("col")
    core = lax.rem(col, 2)
    chip = lax.div(col, 2)
    peer = col + 1 - 2 * core
    assert C % 2 == 0 and C & (C - 1) == 0 and R & (R - 1) == 0

    def col_partner(m):
        return flip(col, m)

    def row_partner(m):
        return flip(row, m)

    def loop(count, body, carry):
        if unroll:
            for n in range(count):
                carry = body(n, carry)
            return carry
        return lax.fori_loop(0, count, body, carry)

    step = -(-T // PARTS)
    for p in range(PARTS):
        lo, hi = p * step, min(T, (p + 1) * step)
        if lo < hi:
            pltpu.make_async_copy(
                tiles_hbm.at[pl.ds(lo, hi - lo)], tiles.at[pl.ds(lo, hi - lo)], tile_sem.at[0]
            ).start()
    if tiles.shape[0] > T:
        tiles[T] = jnp.zeros((B, B), bf16)

    barrier = pltpu.get_barrier_semaphore()
    for m in range(1, C):
        pl.semaphore_signal(
            barrier, inc=1, device_id={"col": col_partner(m)}, device_id_type=pl.DeviceIdType.MESH
        )
    for m in range(1, R):
        pl.semaphore_signal(
            barrier, inc=1, device_id={"row": row_partner(m)}, device_id_type=pl.DeviceIdType.MESH
        )
    mine = label_ref[...]
    lab[col] = jnp.broadcast_to(mine, (8, B))
    pl.semaphore_wait(barrier, C - 1 + R - 1)

    def send(src, dst, send_sem, recv_sem, where):
        pltpu.make_async_remote_copy(
            src_ref=src, dst_ref=dst, send_sem=send_sem, recv_sem=recv_sem,
            device_id=where, device_id_type=pl.DeviceIdType.MESH,
        ).start()

    def landed(ref, recv_sem):
        pltpu.make_async_remote_copy(
            src_ref=ref, dst_ref=ref, send_sem=tile_sem.at[0], recv_sem=recv_sem,
            device_id={"col": peer}, device_id_type=pl.DeviceIdType.MESH,
        ).wait_recv()

    def drained(ref, send_sem):
        pltpu.make_async_remote_copy(
            src_ref=ref, dst_ref=ref, send_sem=send_sem, recv_sem=tile_sem.at[0],
            device_id={"col": peer}, device_id_type=pl.DeviceIdType.MESH,
        ).wait_send()

    def other_chip(j):
        upper = lax.div(2 * chip, Z)
        low = chip + upper * (Z - 1 - 2 * chip)
        far = Z - 1 - j - lax.div(low + j + 1, Z)
        return far + upper * (Z - 1 - 2 * far)

    def tile_at(source, k):
        return tiles[pos[source * R + k]]

    def fold(product):
        folded = product[:, :K]
        for lane in range(K, B, K):
            folded = folded + product[:, lane : lane + K]
        return folded

    def sums_row(products):
        rows = []
        for lo in range(0, len(products), Q):
            part = [fold(p) for p in products[lo : lo + Q]]
            if len(part) < Q:
                part.append(jnp.zeros((K - H * len(part), K), f32))
            rows.append(jnp.sum(jnp.concatenate(part, axis=0).T, axis=0, keepdims=True))
        return rows

    def spread(rows, count):
        values = []
        for q in range(count):
            if q % Q == 0:
                square = jnp.broadcast_to(rows[q // Q], (K, K)).T
            values.append(square[q % Q * H : (q % Q + 1) * H])
        return values

    def wide(value):
        return jnp.concatenate([value] * (B // K), axis=1)

    def encode(t, value):
        top = jnp.clip(jnp.max(jnp.abs(value), axis=0, keepdims=True), 2.0**-100, 2.0**120)
        power = jnp.ceil(jnp.log2(top))
        whole = jnp.round(value * (jnp.exp2(-power) * LIMIT)).astype(i32)
        code[t, col] = (whole[:G] << 16) | (whole[G:] & 0xFFFF)
        unit[t, col] = jnp.exp2(power) * (1.0 / LIMIT)

    def decode(t, c):
        word = code[t, c]
        scale = unit[t, c]
        high = (word >> 16).astype(f32) * scale
        low = ((word << 16) >> 16).astype(f32) * scale
        return jnp.concatenate([high, low], axis=0)

    for m in range(C - 1, 0, -1):
        send(lab.at[col], lab.at[col], lab_send.at[0], lab_recv.at[col], {"col": col_partner(m)})
    class_axis = lax.broadcasted_iota(i32, (K, B), 0)
    ones = jnp.ones((PAD, B), bf16)

    def show(c):
        value = jnp.where(lab[c][0:1] == class_axis, 1.0, 0.0).astype(bf16)
        hot[c] = jnp.concatenate([ones, value], axis=0)

    show(col)
    free = jnp.broadcast_to(mine, (H, B)) < 0
    pltpu.make_async_copy(tiles, tiles, tile_sem.at[0]).wait() if tiles.shape[0] == T else pltpu.make_async_copy(
        tiles.at[pl.ds(0, T)], tiles.at[pl.ds(0, T)], tile_sem.at[0]
    ).wait()

    bounds = [0, min(2, C), min(6, C), C]
    for lo, hi in zip(bounds, bounds[1:]):
        for m in range(max(lo, 1), hi):
            c = col_partner(m)
            landed(lab.at[c], lab_recv.at[c])
            show(c)
        if hi > lo:
            for m in range(R - 1, -1, -1):
                k = row_partner(m)
                value = None if lo == 0 else acc0[k]
                for n in range(lo, hi):
                    c = col_partner(n) if n else col
                    part = jnp.dot(hot[c], tile_at(c, k), preferred_element_type=f32)
                    value = part if value is None else value + part
                acc0[k] = value

    def first_rows(h):
        return (PAD - DEG, H + DEG) if h == 0 else (PAD + h * H, H)

    for h in range(CHAINS):
        lo, size = first_rows(h)
        for m in range(R - 1, 0, -1):
            k = row_partner(m)
            send(
                acc0.at[k, pl.ds(lo, size)], rs0.at[h, m - 1, pl.ds(0, size)],
                deg_send.at[0] if h == 0 else rs0_send.at[0], rs0_recv.at[h], {"row": k},
            )

    def gather_start(t):
        own = code.at[t, col]
        for j in range(Z - 1):
            send(own, own, code_send.at[0], code_recv.at[t, chip], {"col": 2 * other_chip(j) + core})
        send(own, own, code_send.at[0], code_recv.at[t, chip], {"col": peer})
        own = unit.at[t, col]
        for m in range(C - 1, 0, -1):
            send(own, own, unit_send.at[0], unit_recv.at[t], {"col": col_partner(m)})

    def gather_relay(t, j):
        z = other_chip(j)
        block = code.at[t, 2 * z + core]
        landed(block, code_recv.at[t, z])
        send(block, block, code_send.at[0], code_recv.at[t, chip], {"col": peer})

    def gather_end(t):
        landed(code.at[t, pl.ds(0, Z)], code_recv.at[t, chip])
        landed(unit.at[t, pl.ds(0, C - 1)], unit_recv.at[t])

    def stats_start(t, rows):
        for i in range(st_a.shape[2]):
            st_a[t, row, i] = rows[i] if i < len(rows) else jnp.zeros((1, K), f32)
        own = st_a.at[t, row]
        for m in range(R - 1, 0, -1):
            send(own, own, sta_send.at[0], sta_recv.at[t], {"row": row_partner(m)})

    def stats_middle(t):
        landed(st_a.at[t, pl.ds(0, R - 1)], sta_recv.at[t])
        st_c[t, col] = jnp.sum(st_a[t], axis=0)
        own = st_c.at[t, col]
        for m in range(C - 1, 0, -1):
            send(own, own, stc_send.at[0], stc_recv.at[t], {"col": col_partner(m)})

    def stats_end(t):
        landed(st_c.at[t, pl.ds(0, C - 1)], stc_recv.at[t])
        return jnp.sum(st_c[t], axis=0)

    def chain(h):
        clock = h * OFFSET
        yield clock
        lo, size = first_rows(h)
        landed(rs0.at[h, :, pl.ds(0, size)], rs0_recv.at[h])
        value = acc0[row, lo : lo + size]
        for m in range(1, R):
            value = value + rs0[h, m - 1, 0:size]
        if h == 0:
            degree[...] = value[:DEG]
            value = value[DEG:]
        rhs = jnp.where(free, value, 0.0)
        encode(h * ITERS, rhs)
        gather_start(h * ITERS)
        answer[h] = jnp.zeros((H, B), f32)
        residual[h] = rhs
        direction[h] = rhs
        norm = alpha = beta = None
        for s in range(ITERS):
            t = h * ITERS + s
            last = s + 1 == ITERS
            yield clock + NEAR
            for j in range(Z - 2, 0, -1):
                gather_relay(t, j)
            if s:
                stats_middle(t - 1)
            yield clock + FAR
            if Z > 1:
                gather_relay(t, 0)
            yield clock + READY
            if s:
                total = stats_end(t - 1)
                if s == 1:
                    di, ii, norm = spread(total, 3)
                    ri = di
                else:
                    di, ri, ii = spread(total, 3)
                alpha = norm / di
                after = norm - 2.0 * alpha * ri + alpha * alpha * ii
                beta = after / norm
                norm = after
                a, b = wide(alpha), wide(beta)
            gather_end(t)

            def refresh(c, carry):
                fresh = decode(t, c)
                if s == 0:
                    rep_r[h, c] = fresh
                else:
                    old = rep_r[h, c]
                    r = old - a * fresh
                    p = r + b * (old if s == 1 else rep_p[h, c])
                    if not last:
                        rep_r[h, c] = r
                        rep_p[h, c] = p
                    fresh = p
                panel[h, c] = fresh.astype(bf16)
                return carry

            loop(C, refresh, 0)
            for m in range(R - 1, -1, -1):
                k = row_partner(m)

                def one(c, value):
                    part = jnp.dot(panel[h, c], tile_at(c, k), preferred_element_type=f32)
                    return part if value is None else value + part

                acc[t, k] = loop(C, one, None if unroll else jnp.zeros((H, B), f32))
                if m:
                    send(acc.at[t, k], rs.at[t, m - 1], rs_send.at[0], rs_recv.at[t], {"row": k})
            if s:
                d = direction[h]
                r = residual[h] - a * image[h]
                answer[h] = answer[h] + a * d
                residual[h] = r
                direction[h] = r + b * d
            clock += PERIOD
            yield clock
            landed(rs.at[t], rs_recv.at[t])
            mixed = acc[t, row]
            for m in range(1, R):
                mixed = mixed + rs[t, m - 1]
            d = direction[h]
            i = jnp.where(free, degree[0:1] * d - mixed, d)
            if not last:
                encode(t + 1, i)
                gather_start(t + 1)
            image[h] = i
            if last:
                products = [d * i]
            else:
                r = residual[h]
                products = [d * i, i * i, r * r] if s == 0 else [d * i, r * i, i * i]
            stats_start(t, sums_row(products))
        yield clock + NEAR
        stats_middle(t)
        yield clock + READY
        (di,) = spread(stats_end(t), 1)
        a = wide(norm / di)
        x_out[:, h * H : (h + 1) * H] = ((8.0 * K) * (answer[h] + a * direction[h])).T
        r_out[:, h * H : (h + 1) * H] = (residual[h] - a * image[h]).T

    queue = []
    for h in range(CHAINS):
        one = chain(h)
        queue.append((next(one), h, one))
    while queue:
        queue.sort(key=lambda entry: entry[:2])
        _, h, one = queue.pop(0)
        when = next(one, None)
        if when is not None:
            queue.append((when, h, one))

    drained(lab.at[pl.ds(0, C - 1)], lab_send.at[0])
    drained(code.at[:, pl.ds(0, C - 1)], code_send.at[0])
    drained(unit.at[:, pl.ds(0, C - 1)], unit_send.at[0])
    drained(rs0.at[0], deg_send.at[0])
    if CHAINS > 1:
        drained(rs0.at[pl.ds(0, CHAINS - 1), :, pl.ds(0, H)], rs0_send.at[0])
    drained(rs, rs_send.at[0])
    drained(st_a.at[:, pl.ds(0, R - 1)], sta_send.at[0])
    drained(st_c.at[:, pl.ds(0, C - 1)], stc_send.at[0])


def solution(mesh):
    R, C = mesh.shape["row"], mesh.shape["col"]

    def shards(tiles, tile_row, tile_col, label_class):
        T, B = tiles.shape[0], tiles.shape[1]
        K, H, N = CLASSES, CLASSES // CHAINS, CHAINS
        place = lax.rem(tile_row, C) * R + lax.div(tile_col, C)
        slot = lax.broadcasted_iota(jnp.int32, (R * C, T), 0)
        index = lax.broadcasted_iota(jnp.int32, (R * C, T), 1)
        held = T if T == R * C else T + 1
        miss = held - 1 if held > T else 0
        pos = jnp.sum(jnp.where(place[None, :] == slot, index - miss, 0), axis=1)
        if miss:
            pos = pos + miss
        f32, bf16, i32 = jnp.float32, jnp.bfloat16, jnp.int32
        dma = pltpu.SemaphoreType.DMA
        vmem = pl.BlockSpec(memory_space=pltpu.VMEM)
        node = pltpu.VMEM((N, H, B), f32)
        steps = N * ITERS
        lines = -(-3 // (K // H))
        return pl.pallas_call(
            functools.partial(kernel, R, C),
            out_shape=(jax.ShapeDtypeStruct((B, K), f32), jax.ShapeDtypeStruct((B, K), f32)),
            in_specs=[
                pl.BlockSpec(memory_space=pltpu.SMEM),
                vmem,
                pl.BlockSpec(memory_space=pl.ANY),
            ],
            out_specs=(vmem, vmem),
            scratch_shapes=[
                pltpu.VMEM((held, B, B), bf16),
                pltpu.VMEM((C, 8, B), i32),
                pltpu.VMEM((C, PAD + K, B), bf16),
                pltpu.VMEM((R, PAD + K, B), f32),
                pltpu.VMEM((N, R - 1, H + DEG, B), f32),
                pltpu.VMEM((steps, C, H // 2, B), i32),
                pltpu.VMEM((steps, C, 1, B), f32),
                pltpu.VMEM((N, C, H, B), bf16),
                pltpu.VMEM((N, C, H, B), f32),
                pltpu.VMEM((N, C, H, B), f32),
                pltpu.VMEM((steps, R, H, B), f32),
                pltpu.VMEM((steps, R - 1, H, B), f32),
                pltpu.VMEM((steps, R, lines, 1, K), f32),
                pltpu.VMEM((steps, C, lines, 1, K), f32),
                pltpu.VMEM((DEG, B), f32),
                node, node, node, node,
                dma((1,)),
                dma((1,)), dma((C,)),
                dma((1,)), dma((steps, C // 2)),
                dma((1,)), dma((steps,)),
                dma((1,)), dma((1,)), dma((N,)),
                dma((1,)), dma((steps,)),
                dma((1,)), dma((steps,)),
                dma((1,)), dma((steps,)),
            ],
            compiler_params=pltpu.CompilerParams(
                collective_id=0, has_side_effects=True, vmem_limit_bytes=63 * 1024 * 1024
            ),
        )(pos.astype(jnp.int32), label_class.reshape(1, B), tiles)

    placed = (P(("row", "col"), None, None),) + (P(("row", "col")),) * 3
    return jax.shard_map(
        shards,
        mesh=mesh,
        in_specs=placed,
        out_specs=(P(("row", "col"), None), P(("row", "col"), None)),
        check_vma=False,
    )
```

time: 90.2 us -> 71.4 us (0.79)
  Pallas kernels: 84.9 us -> 66.1 us
    pallas_call x1, Pallas kernels: 84.9 us -> 66.1 us  [shards(): pl.pallas_call(functools.partial(kernel, R, C), out_shape=(jax.ShapeDtype...]
where the time goes in v1:
time: 71.4 us; the launch traced here: 71.2 us
  Pallas kernels  66.1 us (93%)
  local copies, waits for them, and re-layouts  3.14 us (4%)
  other arithmetic  1.31 us (2%)
    pallas_call x1, Pallas kernels, shards(): pl.pallas_call(functools.partial(kernel, R, C), out_shape=(jax.ShapeDtype...  66.1 us
    unnamed x2, local copies, waits for them, and re-layouts  3.14 us

profile of v1, /device:TPU:0, one launch (start us, length us, event | category | flops | bytes accessed | tf_op | source)
XLA Modules:
  0.0 71.2 jit_solution(10668631136473312227)
XLA Ops:
  0.6 0.7 fusion.2
  1.3 0.6 select_reduce_fusion.pos
  1.9 66.1 %shard_map.59 = (f32[256,128]{1,0:T(8,128)}, f32[256,128]{1,0:T(8,128)}) custom-call(s32[32]{0:T(128)} %select_reduce_fusion.pos, s32[1,256]{1,0:T(1,128)} %bitcast.1, bf16[32,256,256]{2,1,0:T(8,128)(2,1)} %tiles_hbm.1), custom_call_target="tpu_custom_call" | custom-call | tf_op jit(solution)/shard_map/pallas_call | solution.py:379
  68.1 1.6 %copy.8 = f32[256,128]{1,0:T(8,128)} copy(f32[256,128]{1,0:T(8,128)} %get-tuple-element.4) | data formatting | bytes 262144
  69.7 1.6 %copy.9 = f32[256,128]{1,0:T(8,128)} copy(f32[256,128]{1,0:T(8,128)} %get-tuple-element.5) | data formatting | bytes 262144

commit v2 on v1

--- a/solution.py
+++ b/solution.py
@@ -15,8 +15,8 @@
 PARTS = 4
 CHAINS = 4
 LIMIT = 32700.0
-OFFSET = 1.4
-NEAR, FAR, READY, PERIOD = 2.8, 5.0, 6.5, 10.2
+OFFSET = 2.5
+NEAR, MID, FAR, READY, PERIOD, SUMS = 2.8, 2.8, 5.0, 6.5, 10.2, 5.8
 
 
 def flip(index, mask):
@@ -30,11 +30,12 @@
 
 
 def kernel(
-    R, C, pos, label_ref, tiles_hbm, x_out, r_out,
-    tiles, lab, hot, acc0, rs0, code, unit, panel, rep_r, rep_p, acc, rs, st_a, st_c,
+    R, C, row_hbm, col_hbm, label_hbm, tiles_hbm, x_out, r_out,
+    tile_row, tile_col, pos, label_ref,
+    tiles, lab, hot, acc0, rs0, code, unit, panel, rep_r, rep_p, acc, rs, st,
     degree, direction, image, residual, answer,
     tile_sem, lab_send, lab_recv, code_send, code_recv, unit_send, unit_recv, deg_send, rs0_send, rs0_recv, rs_send, rs_recv,
-    sta_send, sta_recv, stc_send, stc_recv,
+    st_send, st_recv, in_sem,
 ):
     T, B = tiles_hbm.shape[0], tiles_hbm.shape[1]
     Z = C // 2
@@ -62,6 +63,23 @@
             return carry
         return lax.fori_loop(0, count, body, carry)
 
+    inputs = [
+        pltpu.make_async_copy(source, target, in_sem.at[n])
+        for n, (source, target) in enumerate(
+            [(label_hbm, label_ref), (row_hbm, tile_row), (col_hbm, tile_col)]
+        )
+    ]
+    for cp in inputs:
+        cp.start()
+    barrier = pltpu.get_barrier_semaphore()
+    for m in range(C - 1, 0, -1):
+        pl.semaphore_signal(
+            barrier, inc=1, device_id={"col": col_partner(m)}, device_id_type=pl.DeviceIdType.MESH
+        )
+    for m in range(R - 1, 0, -1):
+        pl.semaphore_signal(
+            barrier, inc=1, device_id={"row": row_partner(m)}, device_id_type=pl.DeviceIdType.MESH
+        )
     step = -(-T // PARTS)
     for p in range(PARTS):
         lo, hi = p * step, min(T, (p + 1) * step)
@@ -71,18 +89,26 @@
             ).start()
     if tiles.shape[0] > T:
         tiles[T] = jnp.zeros((B, B), bf16)
-
-    barrier = pltpu.get_barrier_semaphore()
-    for m in range(1, C):
-        pl.semaphore_signal(
-            barrier, inc=1, device_id={"col": col_partner(m)}, device_id_type=pl.DeviceIdType.MESH
-        )
-    for m in range(1, R):
-        pl.semaphore_signal(
-            barrier, inc=1, device_id={"row": row_partner(m)}, device_id_type=pl.DeviceIdType.MESH
-        )
+    for cp in inputs:
+        cp.wait()
     mine = label_ref[...]
-    lab[col] = jnp.broadcast_to(mine, (8, B))
+    lab[col] = mine
+
+    def place(n, carry):
+        tile_row[n] = lax.rem(tile_row[n], C) * R + lax.div(tile_col[n], C)
+        return carry
+
+    lax.fori_loop(0, T, place, 0)
+    miss = tiles.shape[0] - 1
+
+    def locate(slot, carry):
+        found = miss
+        for n in range(T):
+            found = jnp.minimum(found, jnp.where(tile_row[n] == slot, n, miss))
+        pos[slot] = found
+        return carry
+
+    lax.fori_loop(0, R * C, locate, 0)
     pl.semaphore_wait(barrier, C - 1 + R - 1)
 
     def send(src, dst, send_sem, recv_sem, where):
@@ -158,7 +184,7 @@
     ones = jnp.ones((PAD, B), bf16)
 
     def show(c):
-        value = jnp.where(lab[c][0:1] == class_axis, 1.0, 0.0).astype(bf16)
+        value = jnp.where(lab[c] == class_axis, 1.0, 0.0).astype(bf16)
         hot[c] = jnp.concatenate([ones, value], axis=0)
 
     show(col)
@@ -214,26 +240,26 @@
         landed(code.at[t, pl.ds(0, Z)], code_recv.at[t, chip])
         landed(unit.at[t, pl.ds(0, C - 1)], unit_recv.at[t])
 
+    me = row * C + col
+
     def stats_start(t, rows):
-        for i in range(st_a.shape[2]):
-            st_a[t, row, i] = rows[i] if i < len(rows) else jnp.zeros((1, K), f32)
-        own = st_a.at[t, row]
-        for m in range(R - 1, 0, -1):
-            send(own, own, sta_send.at[0], sta_recv.at[t], {"row": row_partner(m)})
-
-    def stats_middle(t):
-        landed(st_a.at[t, pl.ds(0, R - 1)], sta_recv.at[t])
-        st_c[t, col] = jnp.sum(st_a[t], axis=0)
-        own = st_c.at[t, col]
-        for m in range(C - 1, 0, -1):
-            send(own, own, stc_send.at[0], stc_recv.at[t], {"col": col_partner(m)})
+        for i in range(st.shape[2]):
+            st[t, me, i] = rows[i] if i < len(rows) else jnp.zeros((1, K), f32)
+        own = st.at[t, me]
+
+        def out(n, carry):
+            other = lax.rem(me + n + 1, R * C)
+            send(own, own, st_send.at[0], st_recv.at[t], {"row": lax.div(other, C), "col": lax.rem(other, C)})
+            return carry
+
+        loop(R * C - 1, out, 0)
 
     def stats_end(t):
-        landed(st_c.at[t, pl.ds(0, C - 1)], stc_recv.at[t])
-        return jnp.sum(st_c[t], axis=0)
+        landed(st.at[t, pl.ds(0, R * C - 1)], st_recv.at[t])
+        return jnp.sum(st[t], axis=0)
 
     def chain(h):
-        clock = h * OFFSET
+        clock = OFFSET * h
         yield clock
         lo, size = first_rows(h)
         landed(rs0.at[h, :, pl.ds(0, size)], rs0_recv.at[h])
@@ -249,17 +275,18 @@
         answer[h] = jnp.zeros((H, B), f32)
         residual[h] = rhs
         direction[h] = rhs
-        norm = alpha = beta = None
+        norm = None
         for s in range(ITERS):
             t = h * ITERS + s
             last = s + 1 == ITERS
-            yield clock + NEAR
-            for j in range(Z - 2, 0, -1):
-                gather_relay(t, j)
-            if s:
-                stats_middle(t - 1)
-            yield clock + FAR
             if Z > 1:
+                yield clock + NEAR
+                gather_relay(t, Z - 2)
+            if Z > 2:
+                yield clock + MID
+                for j in range(Z - 3, 0, -1):
+                    gather_relay(t, j)
+                yield clock + FAR
                 gather_relay(t, 0)
             yield clock + READY
             if s:
@@ -292,6 +319,13 @@
                 return carry
 
             loop(C, refresh, 0)
+
+            def ship(m, k, value):
+                acc[t, k] = value
+                if m:
+                    send(acc.at[t, k], rs.at[t, m - 1], rs_send.at[0], rs_recv.at[t], {"row": k})
+
+            held = None
             for m in range(R - 1, -1, -1):
                 k = row_partner(m)
 
@@ -299,9 +333,11 @@
                     part = jnp.dot(panel[h, c], tile_at(c, k), preferred_element_type=f32)
                     return part if value is None else value + part
 
-                acc[t, k] = loop(C, one, None if unroll else jnp.zeros((H, B), f32))
-                if m:
-                    send(acc.at[t, k], rs.at[t, m - 1], rs_send.at[0], rs_recv.at[t], {"row": k})
+                value = loop(C, one, None if unroll else jnp.zeros((H, B), f32))
+                if held is not None:
+                    ship(*held)
+                held = (m, k, value)
+            ship(*held)
             if s:
                 d = direction[h]
                 r = residual[h] - a * image[h]
@@ -326,9 +362,7 @@
                 r = residual[h]
                 products = [d * i, i * i, r * r] if s == 0 else [d * i, r * i, i * i]
             stats_start(t, sums_row(products))
-        yield clock + NEAR
-        stats_middle(t)
-        yield clock + READY
+        yield clock + SUMS
         (di,) = spread(stats_end(t), 1)
         a = wide(norm / di)
         x_out[:, h * H : (h + 1) * H] = ((8.0 * K) * (answer[h] + a * direction[h])).T
@@ -352,8 +386,7 @@
     if CHAINS > 1:
         drained(rs0.at[pl.ds(0, CHAINS - 1), :, pl.ds(0, H)], rs0_send.at[0])
     drained(rs, rs_send.at[0])
-    drained(st_a.at[:, pl.ds(0, R - 1)], sta_send.at[0])
-    drained(st_c.at[:, pl.ds(0, C - 1)], stc_send.at[0])
+    drained(st.at[:, pl.ds(0, R * C - 1)], st_send.at[0])
 
 
 def solution(mesh):
@@ -362,17 +395,11 @@
     def shards(tiles, tile_row, tile_col, label_class):
         T, B = tiles.shape[0], tiles.shape[1]
         K, H, N = CLASSES, CLASSES // CHAINS, CHAINS
-        place = lax.rem(tile_row, C) * R + lax.div(tile_col, C)
-        slot = lax.broadcasted_iota(jnp.int32, (R * C, T), 0)
-        index = lax.broadcasted_iota(jnp.int32, (R * C, T), 1)
         held = T if T == R * C else T + 1
-        miss = held - 1 if held > T else 0
-        pos = jnp.sum(jnp.where(place[None, :] == slot, index - miss, 0), axis=1)
-        if miss:
-            pos = pos + miss
         f32, bf16, i32 = jnp.float32, jnp.bfloat16, jnp.int32
         dma = pltpu.SemaphoreType.DMA
-        vmem = pl.BlockSpec(memory_space=pltpu.VMEM)
+        vmem, hbm = pl.BlockSpec(memory_space=pltpu.VMEM), pl.BlockSpec(memory_space=pltpu.HBM)
+        smem = pltpu.SMEM
         node = pltpu.VMEM((N, H, B), f32)
         steps = N * ITERS
         lines = -(-3 // (K // H))
@@ -380,14 +407,13 @@
             functools.partial(kernel, R, C),
             out_shape=(jax.ShapeDtypeStruct((B, K), f32), jax.ShapeDtypeStruct((B, K), f32)),
             in_specs=[
-                pl.BlockSpec(memory_space=pltpu.SMEM),
-                vmem,
-                pl.BlockSpec(memory_space=pl.ANY),
+                hbm, hbm, hbm, hbm,
             ],
             out_specs=(vmem, vmem),
             scratch_shapes=[
+                smem((T,), i32), smem((T,), i32), smem((R * C,), i32), pltpu.VMEM((1, B), i32),
                 pltpu.VMEM((held, B, B), bf16),
-                pltpu.VMEM((C, 8, B), i32),
+                pltpu.VMEM((C, 1, B), i32),
                 pltpu.VMEM((C, PAD + K, B), bf16),
                 pltpu.VMEM((R, PAD + K, B), f32),
                 pltpu.VMEM((N, R - 1, H + DEG, B), f32),
@@ -398,8 +424,7 @@
                 pltpu.VMEM((N, C, H, B), f32),
                 pltpu.VMEM((steps, R, H, B), f32),
                 pltpu.VMEM((steps, R - 1, H, B), f32),
-                pltpu.VMEM((steps, R, lines, 1, K), f32),
-                pltpu.VMEM((steps, C, lines, 1, K), f32),
+                pltpu.VMEM((steps, R * C, lines, 1, K), f32),
                 pltpu.VMEM((DEG, B), f32),
                 node, node, node, node,
                 dma((1,)),
@@ -409,12 +434,12 @@
                 dma((1,)), dma((1,)), dma((N,)),
                 dma((1,)), dma((steps,)),
                 dma((1,)), dma((steps,)),
-                dma((1,)), dma((steps,)),
+                dma((3,)),
             ],
             compiler_params=pltpu.CompilerParams(
-                collective_id=0, has_side_effects=True, vmem_limit_bytes=63 * 1024 * 1024
+                collective_id=0, has_side_effects=True, vmem_limit_bytes=40 * 1024 * 1024
             ),
-        )(pos.astype(jnp.int32), label_class.reshape(1, B), tiles)
+        )(*(pltpu.with_memory_space_constraint(v, pltpu.HBM) for v in (tile_row, tile_col, label_class.reshape(1, B), tiles)))
 
     placed = (P(("row", "col"), None, None),) + (P(("row", "col")),) * 3
     return jax.shard_map(

time: 71.4 us -> 58.9 us (0.82)
  Pallas kernels: 66.1 us -> 56.8 us
  local copies, waits for them, and re-layouts: 3.14 us -> 1.31 us
  other arithmetic: 1.31 us -> 0 us
    pallas_call x1, Pallas kernels: 66.1 us -> 56.8 us  [shards(): pl.pallas_call(functools.partial(kernel, R, C), out_shape=(jax.ShapeDtype...]
    unnamed x2, local copies, waits for them, and re-layouts: 3.14 us -> 1.31 us
where the time goes in v2:
time: 58.9 us; the launch traced here: 58.7 us
  Pallas kernels  56.8 us (96%)
  local copies, waits for them, and re-layouts  1.31 us (2%)
  between operations  0.64 us (1%)
    pallas_call x1, Pallas kernels, shards(): pl.pallas_call(functools.partial(kernel, R, C), out_shape=(jax.ShapeDtype...  56.8 us
    unnamed x2, local copies, waits for them, and re-layouts  1.31 us

profile of v2, /device:TPU:0, one launch (start us, length us, event | category | flops | bytes accessed | tf_op | source)
XLA Modules:
  0.0 58.7 jit_solution(3633534595126967546)
XLA Ops:
  0.6 56.8 %shard_map.59 = (f32[256,128]{1,0:T(8,128)S(1)}, f32[256,128]{1,0:T(8,128)S(1)}) custom-call(s32[32]{0:T(128)} %row_hbm.1, s32[32]{0:T(128)} %col_hbm.1, s32[1,256]{1,0:T(1,128)} %bitcast.1, bf16[32,256,256]{2,1,0:T(8,128)(2,1)} %tiles_hbm.1), custom_call_target="tpu_custom_call" | custom-call | tf_op jit(solution)/shard_map/pallas_call | solution.py:406
  57.4 0.7 %copy.8 = f32[256,128]{1,0:T(8,128)} copy(f32[256,128]{1,0:T(8,128)S(1)} %get-tuple-element.4) | data formatting | bytes 262144
  58.1 0.7 %copy.9 = f32[256,128]{1,0:T(8,128)} copy(f32[256,128]{1,0:T(8,128)S(1)} %get-tuple-element.5) | data formatting | bytes 262144

commit v3 on v2

--- a/solution.py
+++ b/solution.py
@@ -14,9 +14,10 @@
 UNROLL = 32
 PARTS = 4
 CHAINS = 4
+EARLY = 2
 LIMIT = 32700.0
-OFFSET = 2.5
-NEAR, MID, FAR, READY, PERIOD, SUMS = 2.8, 2.8, 5.0, 6.5, 10.2, 5.8
+OFFSET = 2.4
+NEAR, MID, FAR, READY, PERIOD, SUMS = 2.9, 3.9, 4.6, 5.5, 9.7, 5.0
 
 
 def flip(index, mask):
@@ -30,11 +31,11 @@
 
 
 def kernel(
-    R, C, row_hbm, col_hbm, label_hbm, tiles_hbm, x_out, r_out,
+    R, C, row_hbm, col_hbm, label_hbm, tiles_hbm, out,
     tile_row, tile_col, pos, label_ref,
-    tiles, lab, hot, acc0, rs0, code, unit, panel, rep_r, rep_p, acc, rs, st,
+    tiles, lab, hot, acc0, rs0, deg, code, unit, panel, rep_r, rep_p, acc, rs, st,
     degree, direction, image, residual, answer,
-    tile_sem, lab_send, lab_recv, code_send, code_recv, unit_send, unit_recv, deg_send, rs0_send, rs0_recv, rs_send, rs_recv,
+    tile_sem, lab_send, lab_recv, code_send, code_recv, unit_send, unit_recv, side_send, side_recv, deg_send, deg_recv, rs0_send, rs0_recv, rs_send, rs_recv,
     st_send, st_recv, in_sem,
 ):
     T, B = tiles_hbm.shape[0], tiles_hbm.shape[1]
@@ -89,26 +90,10 @@
             ).start()
     if tiles.shape[0] > T:
         tiles[T] = jnp.zeros((B, B), bf16)
-    for cp in inputs:
-        cp.wait()
+    inputs[0].wait()
     mine = label_ref[...]
     lab[col] = mine
 
-    def place(n, carry):
-        tile_row[n] = lax.rem(tile_row[n], C) * R + lax.div(tile_col[n], C)
-        return carry
-
-    lax.fori_loop(0, T, place, 0)
-    miss = tiles.shape[0] - 1
-
-    def locate(slot, carry):
-        found = miss
-        for n in range(T):
-            found = jnp.minimum(found, jnp.where(tile_row[n] == slot, n, miss))
-        pos[slot] = found
-        return carry
-
-    lax.fori_loop(0, R * C, locate, 0)
     pl.semaphore_wait(barrier, C - 1 + R - 1)
 
     def send(src, dst, send_sem, recv_sem, where):
@@ -178,8 +163,31 @@
         low = ((word << 16) >> 16).astype(f32) * scale
         return jnp.concatenate([high, low], axis=0)
 
+    bounds = [0, min(2, C), min(6, C), C]
+
+    def level(m):
+        return sum(m >= bound for bound in bounds[1:])
+
     for m in range(C - 1, 0, -1):
-        send(lab.at[col], lab.at[col], lab_send.at[0], lab_recv.at[col], {"col": col_partner(m)})
+        send(lab.at[col], lab.at[col], lab_send.at[0], lab_recv.at[level(m)], {"col": col_partner(m)})
+    for cp in inputs[1:]:
+        cp.wait()
+
+    def place(n, carry):
+        tile_row[n] = lax.rem(tile_row[n], C) * R + lax.div(tile_col[n], C)
+        return carry
+
+    lax.fori_loop(0, T, place, 0)
+    miss = tiles.shape[0] - 1
+
+    def locate(slot, carry):
+        found = miss
+        for n in range(T):
+            found = jnp.minimum(found, jnp.where(tile_row[n] == slot, n, miss))
+        pos[slot] = found
+        return carry
+
+    lax.fori_loop(0, R * C, locate, 0)
     class_axis = lax.broadcasted_iota(i32, (K, B), 0)
     ones = jnp.ones((PAD, B), bf16)
 
@@ -193,12 +201,11 @@
         tiles.at[pl.ds(0, T)], tiles.at[pl.ds(0, T)], tile_sem.at[0]
     ).wait()
 
-    bounds = [0, min(2, C), min(6, C), C]
-    for lo, hi in zip(bounds, bounds[1:]):
+    for group, (lo, hi) in enumerate(zip(bounds, bounds[1:])):
+        if hi > max(lo, 1):
+            landed(lab.at[pl.ds(0, hi - max(lo, 1))], lab_recv.at[group])
         for m in range(max(lo, 1), hi):
-            c = col_partner(m)
-            landed(lab.at[c], lab_recv.at[c])
-            show(c)
+            show(col_partner(m))
         if hi > lo:
             for m in range(R - 1, -1, -1):
                 k = row_partner(m)
@@ -209,36 +216,48 @@
                     value = part if value is None else value + part
                 acc0[k] = value
 
-    def first_rows(h):
-        return (PAD - DEG, H + DEG) if h == 0 else (PAD + h * H, H)
-
     for h in range(CHAINS):
-        lo, size = first_rows(h)
         for m in range(R - 1, 0, -1):
             k = row_partner(m)
-            send(
-                acc0.at[k, pl.ds(lo, size)], rs0.at[h, m - 1, pl.ds(0, size)],
-                deg_send.at[0] if h == 0 else rs0_send.at[0], rs0_recv.at[h], {"row": k},
-            )
+            send(acc0.at[k, pl.ds(PAD + h * H, H)], rs0.at[h, m - 1], rs0_send.at[0], rs0_recv.at[h], {"row": k})
+    for m in range(R - 1, 0, -1):
+        k = row_partner(m)
+        send(acc0.at[k, pl.ds(PAD - DEG, DEG)], deg.at[m - 1], deg_send.at[0], deg_recv.at[0], {"row": k})
+
+    lead = CHAINS - EARLY
+
+    def slot(t):
+        return t // ITERS * 2 + t % ITERS % 2
 
     def gather_start(t):
+        early = t // ITERS >= lead
         own = code.at[t, col]
         for j in range(Z - 1):
-            send(own, own, code_send.at[0], code_recv.at[t, chip], {"col": 2 * other_chip(j) + core})
-        send(own, own, code_send.at[0], code_recv.at[t, chip], {"col": peer})
+            send(own, own, code_send.at[0], code_recv.at[slot(t), chip], {"col": 2 * other_chip(j) + core})
+        send(own, own, code_send.at[0], code_recv.at[slot(t), chip], {"col": peer})
+        if early:
+            for m in range(R - 1, 0, -1):
+                send(own, code.at[t, C + row], side_send.at[0], side_recv.at[slot(t - lead * ITERS)], {"row": row_partner(m)})
         own = unit.at[t, col]
         for m in range(C - 1, 0, -1):
-            send(own, own, unit_send.at[0], unit_recv.at[t], {"col": col_partner(m)})
+            send(own, own, unit_send.at[0], unit_recv.at[slot(t)], {"col": col_partner(m)})
+        if early:
+            for m in range(R - 1, 0, -1):
+                send(own, unit.at[t, C + row], side_send.at[1], unit_recv.at[slot(t)], {"row": row_partner(m)})
 
     def gather_relay(t, j):
         z = other_chip(j)
         block = code.at[t, 2 * z + core]
-        landed(block, code_recv.at[t, z])
-        send(block, block, code_send.at[0], code_recv.at[t, chip], {"col": peer})
+        landed(block, code_recv.at[slot(t), z])
+        send(block, block, code_send.at[0], code_recv.at[slot(t), chip], {"col": peer})
 
     def gather_end(t):
-        landed(code.at[t, pl.ds(0, Z)], code_recv.at[t, chip])
-        landed(unit.at[t, pl.ds(0, C - 1)], unit_recv.at[t])
+        landed(code.at[t, pl.ds(0, Z)], code_recv.at[slot(t), chip])
+        if t // ITERS >= lead:
+            landed(code.at[t, pl.ds(0, R - 1)], side_recv.at[slot(t - lead * ITERS)])
+            landed(unit.at[t, pl.ds(0, C + R - 2)], unit_recv.at[slot(t)])
+        else:
+            landed(unit.at[t, pl.ds(0, C - 1)], unit_recv.at[slot(t)])
 
     me = row * C + col
 
@@ -249,26 +268,40 @@
 
         def out(n, carry):
             other = lax.rem(me + n + 1, R * C)
-            send(own, own, st_send.at[0], st_recv.at[t], {"row": lax.div(other, C), "col": lax.rem(other, C)})
+            send(own, own, st_send.at[0], st_recv.at[slot(t)], {"row": lax.div(other, C), "col": lax.rem(other, C)})
             return carry
 
-        loop(R * C - 1, out, 0)
+        if unroll:
+            pairs = [(y, z) for y in range(R) for z in range(C)][1:]
+            for y, z in sorted(pairs, key=lambda pair: -(pair[0].bit_count() + pair[1] // 2)):
+                send(own, own, st_send.at[0], st_recv.at[slot(t)], {"row": row_partner(y), "col": col_partner(z)})
+        else:
+            lax.fori_loop(0, R * C - 1, out, 0)
 
     def stats_end(t):
-        landed(st.at[t, pl.ds(0, R * C - 1)], st_recv.at[t])
+        landed(st.at[t, pl.ds(0, R * C - 1)], st_recv.at[slot(t)])
         return jnp.sum(st[t], axis=0)
+
+    def weigh():
+        landed(deg, deg_recv.at[0])
+        value = acc0[row, PAD - DEG : PAD]
+        for m in range(1, R):
+            value = value + deg[m - 1]
+        degree[...] = value
+
+    def apply(t, d):
+        mixed = acc[t, row]
+        for m in range(1, R):
+            mixed = mixed + rs[t, m - 1]
+        return jnp.where(free, degree[0:1] * d - mixed, d)
 
     def chain(h):
         clock = OFFSET * h
         yield clock
-        lo, size = first_rows(h)
-        landed(rs0.at[h, :, pl.ds(0, size)], rs0_recv.at[h])
-        value = acc0[row, lo : lo + size]
+        landed(rs0.at[h], rs0_recv.at[h])
+        value = acc0[row, PAD + h * H : PAD + (h + 1) * H]
         for m in range(1, R):
-            value = value + rs0[h, m - 1, 0:size]
-        if h == 0:
-            degree[...] = value[:DEG]
-            value = value[DEG:]
+            value = value + rs0[h, m - 1]
         rhs = jnp.where(free, value, 0.0)
         encode(h * ITERS, rhs)
         gather_start(h * ITERS)
@@ -303,7 +336,7 @@
                 a, b = wide(alpha), wide(beta)
             gather_end(t)
 
-            def refresh(c, carry):
+            def refresh(c, carry, side=False):
                 fresh = decode(t, c)
                 if s == 0:
                     rep_r[h, c] = fresh
@@ -313,9 +346,11 @@
                     p = r + b * (old if s == 1 else rep_p[h, c])
                     if not last:
                         rep_r[h, c] = r
+                    if side or not last:
                         rep_p[h, c] = p
                     fresh = p
-                panel[h, c] = fresh.astype(bf16)
+                if not side:
+                    panel[h, c] = fresh.astype(bf16)
                 return carry
 
             loop(C, refresh, 0)
@@ -323,7 +358,7 @@
             def ship(m, k, value):
                 acc[t, k] = value
                 if m:
-                    send(acc.at[t, k], rs.at[t, m - 1], rs_send.at[0], rs_recv.at[t], {"row": k})
+                    send(acc.at[t, k], rs.at[t, m - 1], rs_send.at[0], rs_recv.at[t // ITERS], {"row": k})
 
             held = None
             for m in range(R - 1, -1, -1):
@@ -338,35 +373,48 @@
                     ship(*held)
                 held = (m, k, value)
             ship(*held)
+            for m in range(1, R if h >= lead else 1):
+                refresh(C + row_partner(m), 0, True)
             if s:
                 d = direction[h]
                 r = residual[h] - a * image[h]
                 answer[h] = answer[h] + a * d
                 residual[h] = r
                 direction[h] = r + b * d
+            if last and h >= lead:
+                d = direction[h]
+                inner = jnp.where(free, degree[0:1] * d, d) * d - d * acc[t, row]
+                for m in range(1, R):
+                    k = row_partner(m)
+                    inner = inner - rep_p[h, C + k] * acc[t, k]
+                stats_start(t, sums_row([inner]))
+                break
             clock += PERIOD
             yield clock
-            landed(rs.at[t], rs_recv.at[t])
-            mixed = acc[t, row]
-            for m in range(1, R):
-                mixed = mixed + rs[t, m - 1]
-            d = direction[h]
-            i = jnp.where(free, degree[0:1] * d - mixed, d)
-            if not last:
-                encode(t + 1, i)
-                gather_start(t + 1)
+            if h == 0 and s == 0:
+                weigh()
+            landed(rs.at[t], rs_recv.at[t // ITERS])
+            i = apply(t, direction[h])
             image[h] = i
+            d, r = direction[h], residual[h]
             if last:
-                products = [d * i]
-            else:
-                r = residual[h]
-                products = [d * i, i * i, r * r] if s == 0 else [d * i, r * i, i * i]
-            stats_start(t, sums_row(products))
-        yield clock + SUMS
+                stats_start(t, sums_row([d * i]))
+                break
+            encode(t + 1, i)
+            gather_start(t + 1)
+            stats_start(t, sums_row([d * i, i * i, r * r] if s == 0 else [d * i, r * i, i * i]))
+        d = direction[h]
+        if h >= lead:
+            yield clock + READY + SUMS
+            landed(rs.at[t], rs_recv.at[t // ITERS])
+            i = apply(t, d)
+        else:
+            yield clock + SUMS
+            i = image[h]
         (di,) = spread(stats_end(t), 1)
         a = wide(norm / di)
-        x_out[:, h * H : (h + 1) * H] = ((8.0 * K) * (answer[h] + a * direction[h])).T
-        r_out[:, h * H : (h + 1) * H] = (residual[h] - a * image[h]).T
+        out[0:B, h * H : (h + 1) * H] = ((8.0 * K) * (answer[h] + a * d)).T
+        out[B : 2 * B, h * H : (h + 1) * H] = (residual[h] - a * i).T
 
     queue = []
     for h in range(CHAINS):
@@ -382,9 +430,11 @@
     drained(lab.at[pl.ds(0, C - 1)], lab_send.at[0])
     drained(code.at[:, pl.ds(0, C - 1)], code_send.at[0])
     drained(unit.at[:, pl.ds(0, C - 1)], unit_send.at[0])
-    drained(rs0.at[0], deg_send.at[0])
-    if CHAINS > 1:
-        drained(rs0.at[pl.ds(0, CHAINS - 1), :, pl.ds(0, H)], rs0_send.at[0])
+    if EARLY:
+        drained(code.at[pl.ds(0, EARLY * ITERS), pl.ds(0, R - 1)], side_send.at[0])
+        drained(unit.at[pl.ds(0, EARLY * ITERS), pl.ds(0, R - 1)], side_send.at[1])
+    drained(deg, deg_send.at[0])
+    drained(rs0, rs0_send.at[0])
     drained(rs, rs_send.at[0])
     drained(st.at[:, pl.ds(0, R * C - 1)], st_send.at[0])
 
@@ -403,43 +453,45 @@
         node = pltpu.VMEM((N, H, B), f32)
         steps = N * ITERS
         lines = -(-3 // (K // H))
-        return pl.pallas_call(
+        both = pl.pallas_call(
             functools.partial(kernel, R, C),
-            out_shape=(jax.ShapeDtypeStruct((B, K), f32), jax.ShapeDtypeStruct((B, K), f32)),
+            out_shape=jax.ShapeDtypeStruct((2 * B, K), f32),
             in_specs=[
                 hbm, hbm, hbm, hbm,
             ],
-            out_specs=(vmem, vmem),
+            out_specs=vmem,
             scratch_shapes=[
                 smem((T,), i32), smem((T,), i32), smem((R * C,), i32), pltpu.VMEM((1, B), i32),
                 pltpu.VMEM((held, B, B), bf16),
                 pltpu.VMEM((C, 1, B), i32),
                 pltpu.VMEM((C, PAD + K, B), bf16),
                 pltpu.VMEM((R, PAD + K, B), f32),
-                pltpu.VMEM((N, R - 1, H + DEG, B), f32),
-                pltpu.VMEM((steps, C, H // 2, B), i32),
-                pltpu.VMEM((steps, C, 1, B), f32),
+                pltpu.VMEM((N, R - 1, H, B), f32),
+                pltpu.VMEM((R - 1, DEG, B), f32),
+                pltpu.VMEM((steps, C + R, H // 2, B), i32),
+                pltpu.VMEM((steps, C + R, 1, B), f32),
                 pltpu.VMEM((N, C, H, B), bf16),
-                pltpu.VMEM((N, C, H, B), f32),
-                pltpu.VMEM((N, C, H, B), f32),
+                pltpu.VMEM((N, C + R, H, B), f32),
+                pltpu.VMEM((N, C + R, H, B), f32),
                 pltpu.VMEM((steps, R, H, B), f32),
                 pltpu.VMEM((steps, R - 1, H, B), f32),
                 pltpu.VMEM((steps, R * C, lines, 1, K), f32),
                 pltpu.VMEM((DEG, B), f32),
                 node, node, node, node,
                 dma((1,)),
-                dma((1,)), dma((C,)),
-                dma((1,)), dma((steps, C // 2)),
-                dma((1,)), dma((steps,)),
-                dma((1,)), dma((1,)), dma((N,)),
-                dma((1,)), dma((steps,)),
-                dma((1,)), dma((steps,)),
+                dma((1,)), dma((3,)),
+                dma((1,)), dma((2 * N, C // 2)),
+                dma((1,)), dma((2 * N,)), dma((2,)), dma((2 * max(EARLY, 1),)),
+                dma((1,)), dma((1,)), dma((1,)), dma((N,)),
+                dma((1,)), dma((N,)),
+                dma((1,)), dma((2 * N,)),
                 dma((3,)),
             ],
             compiler_params=pltpu.CompilerParams(
                 collective_id=0, has_side_effects=True, vmem_limit_bytes=40 * 1024 * 1024
             ),
         )(*(pltpu.with_memory_space_constraint(v, pltpu.HBM) for v in (tile_row, tile_col, label_class.reshape(1, B), tiles)))
+        return both[:B], both[B:]
 
     placed = (P(("row", "col"), None, None),) + (P(("row", "col")),) * 3
     return jax.shard_map(

time: 58.9 us -> 52.8 us (0.90)
  Pallas kernels: 56.8 us -> 51.3 us
  local copies, waits for them, and re-layouts: 1.31 us -> 0.72 us
    pallas_call x1, Pallas kernels: 56.8 us -> 51.3 us  [shards(): pl.pallas_call(functools.partial(kernel, R, C), out_shape=jax.ShapeDtypeS...]
    unnamed x2 -> x0, local copies, waits for them, and re-layouts: 1.31 us -> none
    slice x0 -> x1, local copies, waits for them, and re-layouts: none -> 0.72 us  [shards(): return (both[:B], both[B:])]
where the time goes in v3:
time: 52.8 us; the launch traced here: 52.6 us
  Pallas kernels  51.3 us (97%)
  local copies, waits for them, and re-layouts  0.72 us (1%)
  between operations  0.64 us (1%)
    pallas_call x1, Pallas kernels, shards(): pl.pallas_call(functools.partial(kernel, R, C), out_shape=jax.ShapeDtypeS...  51.3 us

profile of v3, /device:TPU:0, one launch (start us, length us, event | category | flops | bytes accessed | tf_op | source)
XLA Modules:
  0.0 52.6 jit_solution(6119813818270241675)
XLA Ops:
  0.6 51.3 %shard_map.59 = f32[512,128]{1,0:T(8,128)S(1)} custom-call(s32[32]{0:T(128)} %row_hbm.1, s32[32]{0:T(128)} %col_hbm.1, s32[1,256]{1,0:T(1,128)} %bitcast.1, bf16[32,256,256]{2,1,0:T(8,128)(2,1)} %tiles_hbm.1), custom_call_target="tpu_custom_call" | custom-call | tf_op jit(solution)/shard_map/pallas_call | solution.py:456
  51.9 0.7 %fusion = (f32[256,128]{1,0:T(8,128)}, f32[256,128]{1,0:T(8,128)}) fusion(f32[512,128]{1,0:T(8,128)S(1)} %shard_map.59), kind=kLoop, calls=%fused_computation | loop fusion | bytes 524288 | tf_op jit(solution)/shard_map/slice | solution.py:494

commit v4 on v3

--- a/solution.py
+++ b/solution.py
@@ -17,7 +17,7 @@
 EARLY = 2
 LIMIT = 32700.0
 OFFSET = 2.4
-NEAR, MID, FAR, READY, PERIOD, SUMS = 2.9, 3.9, 4.6, 5.5, 9.7, 5.0
+NEAR, MID, FAR, READY, PERIOD, SUMS = 2.9, 3.9, 4.4, 4.9, 9.3, 4.5
 
 
 def flip(index, mask):
@@ -33,9 +33,9 @@
 def kernel(
     R, C, row_hbm, col_hbm, label_hbm, tiles_hbm, out,
     tile_row, tile_col, pos, label_ref,
-    tiles, lab, hot, acc0, rs0, deg, code, unit, panel, rep_r, rep_p, acc, rs, st,
+    tiles, lab, hot, acc0, rs0, deg, code, unit, panel, rep_r, rep_p, acc, piece, grade, rs, rg, st,
     degree, direction, image, residual, answer,
-    tile_sem, lab_send, lab_recv, code_send, code_recv, unit_send, unit_recv, side_send, side_recv, deg_send, deg_recv, rs0_send, rs0_recv, rs_send, rs_recv,
+    tile_sem, lab_send, lab_recv, code_send, code_recv, unit_send, unit_recv, side_send, side_recv, deg_send, deg_recv, rs0_send, rs0_recv, rs_send, rs_recv, rg_send, rg_recv,
     st_send, st_recv, in_sem,
 ):
     T, B = tiles_hbm.shape[0], tiles_hbm.shape[1]
@@ -149,16 +149,19 @@
     def wide(value):
         return jnp.concatenate([value] * (B // K), axis=1)
 
-    def encode(t, value):
+    def pack(value):
         top = jnp.clip(jnp.max(jnp.abs(value), axis=0, keepdims=True), 2.0**-100, 2.0**120)
         power = jnp.ceil(jnp.log2(top))
         whole = jnp.round(value * (jnp.exp2(-power) * LIMIT)).astype(i32)
-        code[t, col] = (whole[:G] << 16) | (whole[G:] & 0xFFFF)
-        unit[t, col] = jnp.exp2(power) * (1.0 / LIMIT)
+        return (whole[:G] << 16) | (whole[G:] & 0xFFFF), jnp.exp2(power) * (1.0 / LIMIT)
+
+    def encode(t, value):
+        code[t, col], unit[t, col] = pack(value)
 
     def decode(t, c):
-        word = code[t, c]
-        scale = unit[t, c]
+        return unpack(code[t, c], unit[t, c])
+
+    def unpack(word, scale):
         high = (word >> 16).astype(f32) * scale
         low = ((word << 16) >> 16).astype(f32) * scale
         return jnp.concatenate([high, low], axis=0)
@@ -290,9 +293,9 @@
         degree[...] = value
 
     def apply(t, d):
-        mixed = acc[t, row]
+        mixed = acc[t // ITERS, row]
         for m in range(1, R):
-            mixed = mixed + rs[t, m - 1]
+            mixed = mixed + unpack(rs[t, m - 1], rg[t, m - 1])
         return jnp.where(free, degree[0:1] * d - mixed, d)
 
     def chain(h):
@@ -356,9 +359,12 @@
             loop(C, refresh, 0)
 
             def ship(m, k, value):
-                acc[t, k] = value
+                if m == 0 or (last and h >= lead):
+                    acc[h, k] = value
                 if m:
-                    send(acc.at[t, k], rs.at[t, m - 1], rs_send.at[0], rs_recv.at[t // ITERS], {"row": k})
+                    piece[t, k], grade[t, k] = pack(value)
+                    send(piece.at[t, k], rs.at[t, m - 1], rs_send.at[0], rs_recv.at[h], {"row": k})
+                    send(grade.at[t, k], rg.at[t, m - 1], rg_send.at[0], rg_recv.at[h], {"row": k})
 
             held = None
             for m in range(R - 1, -1, -1):
@@ -383,17 +389,18 @@
                 direction[h] = r + b * d
             if last and h >= lead:
                 d = direction[h]
-                inner = jnp.where(free, degree[0:1] * d, d) * d - d * acc[t, row]
+                inner = jnp.where(free, degree[0:1] * d, d) * d - d * acc[h, row]
                 for m in range(1, R):
                     k = row_partner(m)
-                    inner = inner - rep_p[h, C + k] * acc[t, k]
+                    inner = inner - rep_p[h, C + k] * acc[h, k]
                 stats_start(t, sums_row([inner]))
                 break
             clock += PERIOD
             yield clock
             if h == 0 and s == 0:
                 weigh()
-            landed(rs.at[t], rs_recv.at[t // ITERS])
+            landed(rs.at[t], rs_recv.at[h])
+            landed(rg.at[t], rg_recv.at[h])
             i = apply(t, direction[h])
             image[h] = i
             d, r = direction[h], residual[h]
@@ -406,7 +413,8 @@
         d = direction[h]
         if h >= lead:
             yield clock + READY + SUMS
-            landed(rs.at[t], rs_recv.at[t // ITERS])
+            landed(rs.at[t], rs_recv.at[h])
+            landed(rg.at[t], rg_recv.at[h])
             i = apply(t, d)
         else:
             yield clock + SUMS
@@ -436,6 +444,7 @@
     drained(deg, deg_send.at[0])
     drained(rs0, rs0_send.at[0])
     drained(rs, rs_send.at[0])
+    drained(rg, rg_send.at[0])
     drained(st.at[:, pl.ds(0, R * C - 1)], st_send.at[0])
 
 
@@ -473,8 +482,11 @@
                 pltpu.VMEM((N, C, H, B), bf16),
                 pltpu.VMEM((N, C + R, H, B), f32),
                 pltpu.VMEM((N, C + R, H, B), f32),
-                pltpu.VMEM((steps, R, H, B), f32),
-                pltpu.VMEM((steps, R - 1, H, B), f32),
+                pltpu.VMEM((N, R, H, B), f32),
+                pltpu.VMEM((steps, R, H // 2, B), i32),
+                pltpu.VMEM((steps, R, 1, B), f32),
+                pltpu.VMEM((steps, R - 1, H // 2, B), i32),
+                pltpu.VMEM((steps, R - 1, 1, B), f32),
                 pltpu.VMEM((steps, R * C, lines, 1, K), f32),
                 pltpu.VMEM((DEG, B), f32),
                 node, node, node, node,
@@ -483,7 +495,7 @@
                 dma((1,)), dma((2 * N, C // 2)),
                 dma((1,)), dma((2 * N,)), dma((2,)), dma((2 * max(EARLY, 1),)),
                 dma((1,)), dma((1,)), dma((1,)), dma((N,)),
-                dma((1,)), dma((N,)),
+                dma((1,)), dma((N,)), dma((1,)), dma((N,)),
                 dma((1,)), dma((2 * N,)),
                 dma((3,)),
             ],

time: 52.8 us -> 50.7 us (0.960)
  Pallas kernels: 51.3 us -> 49.1 us
    pallas_call x1, Pallas kernels: 51.3 us -> 49.1 us  [shards(): pl.pallas_call(functools.partial(kernel, R, C), out_shape=jax.ShapeDtypeS...]
where the time goes in v4:
time: 50.7 us; the launch traced here: 50.5 us
  Pallas kernels  49.1 us (97%)
  local copies, waits for them, and re-layouts  0.72 us (1%)
  between operations  0.64 us (1%)
    pallas_call x1, Pallas kernels, shards(): pl.pallas_call(functools.partial(kernel, R, C), out_shape=jax.ShapeDtypeS...  49.1 us

profile of v4, /device:TPU:0, one launch (start us, length us, event | category | flops | bytes accessed | tf_op | source)
XLA Modules:
  0.0 50.5 jit_solution(3447611563557259204)
XLA Ops:
  0.6 49.1 %shard_map.59 = f32[512,128]{1,0:T(8,128)S(1)} custom-call(s32[32]{0:T(128)} %row_hbm.1, s32[32]{0:T(128)} %col_hbm.1, s32[1,256]{1,0:T(1,128)} %bitcast.1, bf16[32,256,256]{2,1,0:T(8,128)(2,1)} %tiles_hbm.1), custom_call_target="tpu_custom_call" | custom-call | tf_op jit(solution)/shard_map/pallas_call | solution.py:465
  49.8 0.7 %fusion = (f32[256,128]{1,0:T(8,128)}, f32[256,128]{1,0:T(8,128)}) fusion(f32[512,128]{1,0:T(8,128)S(1)} %shard_map.59), kind=kLoop, calls=%fused_computation | loop fusion | bytes 524288 | tf_op jit(solution)/shard_map/slice | solution.py:506

commit v5 on v4

--- a/solution.py
+++ b/solution.py
@@ -16,8 +16,8 @@
 CHAINS = 4
 EARLY = 2
 LIMIT = 32700.0
-OFFSET = 2.4
-NEAR, MID, FAR, READY, PERIOD, SUMS = 2.9, 3.9, 4.4, 4.9, 9.3, 4.5
+OFFSET = 2.2
+NEAR, MID, FAR, READY, PERIOD, SUMS = 2.9, 3.6, 4.3, 4.9, 8.8, 4.3
 
 
 def flip(index, mask):

time: 50.7 us -> 50.7 us (level)
  no operation moved by 1% of the time
where the time goes in v5:
time: 50.7 us; the launch traced here: 50.5 us
  Pallas kernels  49.1 us (97%)
  local copies, waits for them, and re-layouts  0.72 us (1%)
  between operations  0.64 us (1%)
    pallas_call x1, Pallas kernels, shards(): pl.pallas_call(functools.partial(kernel, R, C), out_shape=jax.ShapeDtypeS...  49.1 us

profile of v5, /device:TPU:0, one launch (start us, length us, event | category | flops | bytes accessed | tf_op | source)
XLA Modules:
  0.0 50.5 jit_solution(3447611563557259204)
XLA Ops:
  0.6 49.1 %shard_map.59 = f32[512,128]{1,0:T(8,128)S(1)} custom-call(s32[32]{0:T(128)} %row_hbm.1, s32[32]{0:T(128)} %col_hbm.1, s32[1,256]{1,0:T(1,128)} %bitcast.1, bf16[32,256,256]{2,1,0:T(8,128)(2,1)} %tiles_hbm.1), custom_call_target="tpu_custom_call" | custom-call | tf_op jit(solution)/shard_map/pallas_call | solution.py:465
  49.8 0.7 %fusion = (f32[256,128]{1,0:T(8,128)}, f32[256,128]{1,0:T(8,128)}) fusion(f32[512,128]{1,0:T(8,128)S(1)} %shard_map.59), kind=kLoop, calls=%fused_computation | loop fusion | bytes 524288 | tf_op jit(solution)/shard_map/slice | solution.py:506
